TPU v7x, 32 devices: a whole 2x2x4 slice. The times are simulated.
32 devices in a mesh: rep: 16 (over z, y, core), tp: 2 (over x).
Axes of the slice: x: 2, y: 2, z: 4, core: 2. Of those that a mesh axis runs over, the one named last changes fastest.
Arguments:
- positions: int32 [4096], P('rep'), may hold values from 0 to 8191
- activations: bfloat16 [4096, 4096], P('rep', 'tp'), may hold values from -6 to 6
- norm_gain: bfloat16 [4096], P('tp'), may hold values from 0.5 to 1.5
- qkv_weight: bfloat16 [4096, 6144], P('rep', 'tp'), may hold values from -0.09375 to 0.09375
- gate_up_weight: bfloat16 [4096, 14336], P('rep', 'tp'), may hold values from -0.09375 to 0.09375
Outputs:
- qkv_out: bfloat16 [4096, 6144], P('rep', 'tp')
- hidden: bfloat16 [4096, 7168], P('rep', 'tp')
All inputs are finite; a program needn't handle non-finite values.
Results may differ from a plain program's by a relative error of at most 0.0058.
Values may be sent and summed in bfloat16 or wider, within the bound.
A program may use at most 192 MiB of HBM per device.

v0:
```python
import functools

import jax
import jax.numpy as jnp
from jax import lax
from jax.experimental import pallas as pl
from jax.experimental.pallas import tpu as pltpu
from jax.sharding import PartitionSpec as P

QH = 32
KVH = 8
HD = 128
MESH = pl.DeviceIdType.MESH
CORES = 2
QUARTERS = 4

theta_base = 500000.0
norm_eps = 1e-05


def normalize(gathered, gain_row):
    values = gathered.astype(jnp.float32)
    mean_square = jnp.mean(values * values, axis=1, keepdims=True)
    return (values * lax.rsqrt(mean_square + norm_eps) * gain_row.astype(jnp.float32)).astype(
        jnp.bfloat16
    )


def angle_parts(positions):
    half_size = HD // 2
    frequency = theta_base ** (-2.0 * jnp.arange(half_size, dtype=jnp.float32) / HD)
    angles = positions.astype(jnp.float32)[:, None] * frequency[None, :]
    return jnp.cos(angles), jnp.sin(angles)


def rotary(joined_qkv, positions):
    row_count = joined_qkv.shape[0]
    per_group = QH // KVH + 2
    half_size = HD // 2
    head_view = joined_qkv.reshape(row_count, -1, per_group, HD)
    cosine, sine_part = angle_parts(positions)
    cosine = cosine[:, None, None, :]
    sine_part = sine_part[:, None, None, :]
    leading = head_view[..., :half_size]
    trailing = head_view[..., half_size:]
    turned = jnp.concatenate(
        [leading * cosine - trailing * sine_part, trailing * cosine + leading * sine_part], axis=-1
    )
    rotated_mask = (jnp.arange(per_group) < per_group - 1)[None, None, :, None]
    return jnp.where(rotated_mask, turned, head_view).reshape(row_count, -1)


def contract_rows(chosen, piece):
    return jnp.dot(chosen, piece, preferred_element_type=jnp.float32)


def plain(positions, activations, norm_gain, qkv_weight, gate_up_weight):
    features, gains = (
        lax.all_gather(activations, "tp", axis=1, tiled=True),
        lax.all_gather(norm_gain, "tp", axis=0, tiled=True),
    )
    normed = normalize(features, gains)
    seq_count = normed.shape[0]
    qkv_partial = contract_rows(normed, lax.all_gather(qkv_weight, "rep", axis=0, tiled=True))
    gateup_partial = contract_rows(
        normed, lax.all_gather(gate_up_weight, "rep", axis=0, tiled=True)
    )
    qkv_out = rotary(qkv_partial, positions).astype(jnp.bfloat16)
    paired = gateup_partial.reshape(seq_count, 2, -1)
    hidden = (jax.nn.silu(paired[:, 0]) * paired[:, 1]).astype(jnp.bfloat16)
    return (qkv_out, hidden)


def widths_of(total):
    blocks = total // HD
    tail = min(3, blocks)
    wide, left = divmod(blocks - tail, QUARTERS)
    return [QUARTERS * HD] * wide + ([left * HD] if left else []) + [HD] * tail


def kernel(plan, table_in, x_in, gain_in, wq_in, wg_in, q_out, h_out, *scratch):
    (chips, seqs, feats, qcols, hcols, widths) = plan
    n_gu = len(widths)
    x_buf, t_buf, g_buf, q_res, wq_buf = scratch[:5]
    gu_bufs = scratch[5 : 5 + n_gu]
    h_res = scratch[5 + n_gu : 5 + 2 * n_gu]
    (w_send, w_recv, f_send, f_recv, o_send, o_recv, a_send, a_recv, l_sem) = scratch[5 + 2 * n_gu :]

    rep, t = lax.axis_index("rep"), lax.axis_index("tp")
    core = rep % CORES
    chip = rep // CORES
    half = chip // QUARTERS
    quarter = chip % QUARTERS
    zl, y = quarter // 2, quarter % 2

    def dev(other_chip, other_core=None, other_t=None):
        return (
            other_chip * CORES + (core if other_core is None else other_core),
            t if other_t is None else other_t,
        )

    sibling = dev(chip, 1 - core)
    across = dev(chip, core, 1 - t)
    z_peer = dev(half * QUARTERS + (1 - zl) * 2 + y)
    y_peer = dev(half * QUARTERS + zl * 2 + (1 - y))

    barrier = pltpu.get_barrier_semaphore()
    for k in range(1, chips):
        pl.semaphore_signal(barrier, inc=1, device_id=dev((chip + k) % chips), device_id_type=MESH)
    pl.semaphore_signal(barrier, inc=1, device_id=sibling, device_id_type=MESH)
    pl.semaphore_signal(barrier, inc=1, device_id=across, device_id_type=MESH)
    pl.semaphore_wait(barrier, chips + 1)

    def remote(src, dst, ssem, rsem, where):
        return pltpu.make_async_remote_copy(
            src_ref=src, dst_ref=dst, send_sem=ssem, recv_sem=rsem, device_id=where, device_id_type=MESH
        )

    def rows(index, count=1):
        return pl.ds(pl.multiple_of(index * seqs, seqs), count * seqs)

    def cols(base, width):
        return pl.ds(pl.multiple_of(base, HD), width)

    slot = y * 2 + zl
    mine = cols(t * feats, feats)
    theirs = cols((1 - t) * feats, feats)
    local = [
        pltpu.make_async_copy(x_in, x_buf.at[rows(slot), mine], l_sem.at[0]),
        pltpu.make_async_copy(table_in, t_buf.at[rows(slot)], l_sem.at[1]),
        pltpu.make_async_copy(gain_in, g_buf.at[mine], l_sem.at[2]),
    ]
    other = y * 2 + (1 - zl)
    z_x = remote(x_in, x_buf.at[rows(slot), mine], a_send.at[0], a_recv.at[0], z_peer)
    z_t = remote(table_in, t_buf.at[rows(slot)], a_send.at[1], a_recv.at[1], z_peer)
    x_own = remote(x_in, x_buf.at[rows(slot), mine], a_send.at[2], a_recv.at[2], across)
    x_gain = remote(gain_in, g_buf.at[mine], a_send.at[3], a_recv.at[3], across)
    y_own = remote(x_in, x_buf.at[rows(slot), mine], a_send.at[4], a_recv.at[4], y_peer)
    y_t = remote(table_in, t_buf.at[rows(slot)], a_send.at[5], a_recv.at[5], y_peer)
    y_two = remote(x_buf.at[rows(other), mine], x_buf.at[rows(other), mine], a_send.at[6], a_recv.at[6], y_peer)
    y_t2 = remote(t_buf.at[rows(other)], t_buf.at[rows(other)], a_send.at[7], a_recv.at[7], y_peer)
    x_two = remote(x_buf.at[rows(other), mine], x_buf.at[rows(other), mine], a_send.at[8], a_recv.at[8], across)
    far = (1 - y) * 2 + zl
    far2 = (1 - y) * 2 + (1 - zl)
    x_three = remote(x_buf.at[rows(far), mine], x_buf.at[rows(far), mine], a_send.at[9], a_recv.at[9], across)
    x_four = remote(x_buf.at[rows(far2), mine], x_buf.at[rows(far2), mine], a_send.at[10], a_recv.at[10], across)

    pieces = [(wq_in, lambda q: q * qcols, qcols, wq_buf, 0)]
    chunks = [[0]]
    at = 0
    for n, width in enumerate(widths):
        for part in range(2):
            base = part * hcols * QUARTERS + at
            pieces.append((wg_in, lambda q, base=base: base + q * hcols, width, gu_bufs[n], part * width))
        chunks.append([2 * n + 1, 2 * n + 2])
        at += width

    def piece_src(p, q):
        src, col, width, _, _ = pieces[p]
        return src.at[:, cols(col(q), width)]

    def piece_dst(p, owner_rep):
        _, _, width, buf, col = pieces[p]
        return buf.at[rows(owner_rep), col : col + width]

    order = [(k + chips // 2) % chips for k in range(chips)]
    order = [k for k in order if k]

    def weight_send(p, k):
        to = (chip + k) % chips
        return remote(
            piece_src(p, to % QUARTERS), piece_dst(p, rep), w_send.at[p, k], w_recv.at[p, chip], dev(to)
        )

    def weight_from(p, k):
        source = (chip + chips - k) % chips
        owner = source * CORES + core
        return remote(
            piece_dst(p, owner), piece_dst(p, owner), w_send.at[p, k], w_recv.at[p, source], dev(source)
        )

    def own_local(p):
        return pltpu.make_async_copy(piece_src(p, quarter), piece_dst(p, rep), l_sem.at[3 + p])

    def own_pass(p):
        return remote(piece_src(p, quarter), piece_dst(p, rep), f_send.at[p, 0], f_recv.at[p, 0], sibling)

    def passed(p, k):
        source = (chip + chips - k) % chips
        owner = source * CORES + core
        return remote(piece_dst(p, owner), piece_dst(p, owner), f_send.at[p, k], f_recv.at[p, k], sibling)

    def passed_in(p, k):
        source = (chip + chips - k) % chips
        owner = source * CORES + (1 - core)
        return remote(piece_dst(p, owner), piece_dst(p, owner), f_send.at[p, k], f_recv.at[p, k], sibling)

    def start_chunk(c):
        for k in order:
            for p in chunks[c]:
                weight_send(p, k).start()
        for p in chunks[c]:
            own_local(p).start()
            own_pass(p).start()

    def pass_chunk(c):
        for k in order:
            for p in chunks[c]:
                weight_from(p, k).wait_recv()
                passed(p, k).start()

    def finish_chunk(c):
        for p in chunks[c]:
            own_local(p).wait()
            for k in range(chips):
                passed_in(p, k).wait_recv()

    for copy in (z_x, z_t, x_own, x_gain, y_own, y_t, *local):
        copy.start()
    start_chunk(0)
    z_x.wait_recv()
    y_two.start()
    x_two.start()
    z_t.wait_recv()
    y_t2.start()
    for c in range(1, len(chunks)):
        start_chunk(c)
    y_own.wait_recv()
    x_three.start()
    y_two.wait_recv()
    x_four.start()
    pass_chunk(0)
    for copy in (y_t, y_t2, x_own, x_gain, x_two, x_three, x_four):
        copy.wait_recv()
    for copy in local:
        copy.wait()
    for copy in (z_x, z_t, x_own, x_gain, y_own, y_t, y_two, y_t2, x_two, x_three, x_four):
        copy.wait_send()

    total = QUARTERS * seqs
    tall = 32

    gain_row = g_buf[...].astype(jnp.float32)[None, :]

    @pl.loop(0, total // tall)
    def _(i):
        at_rows = pl.ds(pl.multiple_of(i * tall, tall), tall)
        values = x_buf[at_rows, :].astype(jnp.float32)
        mean_square = jnp.mean(values * values, axis=1, keepdims=True)
        x_buf[at_rows, :] = (values * lax.rsqrt(mean_square + norm_eps) * gain_row).astype(jnp.bfloat16)

    per_group = QH // KVH + 2
    deep = 2 * seqs

    def compute(c):
        @pl.loop(0, total // deep)
        def _(i):
            at_rows = pl.ds(pl.multiple_of(i * deep, deep), deep)
            chosen = x_buf[at_rows, :]
            if c == 0:
                table = t_buf[at_rows, :]
                swapped = pltpu.roll(table, HD // 2, 1)
                lane = lax.broadcasted_iota(jnp.int32, table.shape, 1)
                low = lane < HD // 2
                cosine = jnp.where(low, table, swapped)
                sine_part = jnp.where(low, -swapped, table)
                for n in range(0, qcols, 2 * HD):
                    wide = jnp.dot(chosen, wq_buf[:, n : n + 2 * HD], preferred_element_type=jnp.float32)
                    for s in range(2):
                        head = wide[:, s * HD : (s + 1) * HD]
                        if (n // HD + s) % per_group < per_group - 1:
                            head = head * cosine + pltpu.roll(head, HD // 2, 1) * sine_part
                        q_res[at_rows, n + s * HD : n + (s + 1) * HD] = head.astype(jnp.bfloat16)
            else:
                width = widths[c - 1]
                both = jnp.dot(chosen, gu_bufs[c - 1][...], preferred_element_type=jnp.float32)
                gate, up = both[:, :width], both[:, width:]
                h_res[c - 1][at_rows, :] = (gate / (1.0 + jnp.exp(-gate)) * up).astype(jnp.bfloat16)

    def result(c, q):
        place = (q % 2) * 2 + q // 2
        if c == 0:
            return q_res.at[rows(place)], lambda mover: q_out.at[:, cols(mover * qcols, qcols)]
        offset = sum(widths[: c - 1])
        return h_res[c - 1].at[rows(place)], lambda mover: h_out.at[:, cols(mover * hcols + offset, widths[c - 1])]

    def out_send(c, k):
        to = (quarter + k) % QUARTERS
        src, dst = result(c, to)
        return remote(src, dst(quarter), o_send.at[c, k], o_recv.at[c, k], dev(half * QUARTERS + to))

    def out_from(c, k):
        source = (quarter + QUARTERS - k) % QUARTERS
        src, dst = result(c, quarter)
        return remote(src, dst(source), o_send.at[c, k], o_recv.at[c, k], dev(half * QUARTERS + source))

    def out_local(c):
        src, dst = result(c, quarter)
        return pltpu.make_async_copy(src, dst(quarter), l_sem.at[3 + len(pieces) + c])

    def ship(c):
        for k in range(1, QUARTERS):
            out_send(c, k).start()
        out_local(c).start()

    for c in range(len(chunks)):
        if c:
            pass_chunk(c)
        finish_chunk(c)
        compute(c)
        ship(c)
        if c + 99 < len(chunks):
            start_chunk(c + 99)

    for c in range(len(chunks)):
        for p in chunks[c]:
            for k in range(1, chips):
                weight_send(p, k).wait_send()
                passed(p, k).wait_send()
            own_pass(p).wait_send()
        out_local(c).wait()
        for k in range(1, QUARTERS):
            out_send(c, k).wait_send()
            out_from(c, k).wait_recv()


def fused(chips, positions, activations, norm_gain, qkv_weight, gate_up_weight):
    seqs, feats = activations.shape
    depth, qkv_cols = qkv_weight.shape
    qcols = qkv_cols // QUARTERS
    hcols = gate_up_weight.shape[1] // 2 // QUARTERS
    widths = widths_of(hcols)
    rank = chips * CORES
    table = jnp.concatenate(angle_parts(positions), axis=1)
    gains = norm_gain
    bf16, f32 = jnp.bfloat16, jnp.float32
    pieces, chunks = 1 + 2 * len(widths), 1 + len(widths)
    dma = pltpu.SemaphoreType.DMA
    scratch = [
        pltpu.VMEM((QUARTERS * seqs, 2 * feats), bf16),
        pltpu.VMEM((QUARTERS * seqs, HD), f32),
        pltpu.VMEM((2 * feats,), bf16),
        pltpu.VMEM((QUARTERS * seqs, qcols), bf16),
        pltpu.VMEM((rank * depth, qcols), bf16),
        *[pltpu.VMEM((rank * depth, 2 * w), bf16) for w in widths],
        *[pltpu.VMEM((QUARTERS * seqs, w), bf16) for w in widths],
        dma((pieces, chips)),
        dma((pieces, chips)),
        dma((pieces, chips)),
        dma((pieces, chips)),
        dma((chunks, QUARTERS)),
        dma((chunks, QUARTERS)),
        dma((11,)),
        dma((11,)),
        dma((3 + pieces + chunks,)),
    ]
    plan = (chips, seqs, feats, qcols, hcols, tuple(widths))
    anywhere = pl.BlockSpec(memory_space=pl.ANY)
    return pl.pallas_call(
        functools.partial(kernel, plan),
        out_shape=(
            pltpu.VMEM((seqs, qkv_cols), bf16),
            pltpu.VMEM((seqs, hcols * QUARTERS), bf16),
        ),
        in_specs=[anywhere] * 5,
        out_specs=(pl.BlockSpec(memory_space=pltpu.VMEM), pl.BlockSpec(memory_space=pltpu.VMEM)),
        scratch_shapes=scratch,
        compiler_params=pltpu.CompilerParams(
            collective_id=0, has_side_effects=True, vmem_limit_bytes=60 * 1024 * 1024
        ),
    )(table, activations, gains, qkv_weight, gate_up_weight)


def per_device(reps, tps, positions, activations, norm_gain, qkv_weight, gate_up_weight):
    chips = reps // CORES
    seqs, depth = activations.shape[0], qkv_weight.shape[0]
    fits = (
        chips == 2 * QUARTERS
        and tps == 2
        and seqs == depth
        and seqs % 32 == 0
        and qkv_weight.shape[1] % (QUARTERS * (QH // KVH + 2) * HD) == 0
        and gate_up_weight.shape[1] % (2 * QUARTERS * HD) == 0
    )
    step = functools.partial(fused, chips) if fits else plain
    return step(positions, activations, norm_gain, qkv_weight, gate_up_weight)


def solution(mesh):
    placed = (P("rep"), P("rep", "tp"), P("tp"), P("rep", "tp"), P("rep", "tp"))
    return jax.shard_map(
        functools.partial(per_device, mesh.shape["rep"], mesh.shape["tp"]),
        mesh=mesh,
        in_specs=placed,
        out_specs=(P("rep", "tp"), P("rep", "tp")),
        check_vma=False,
    )
```

profile of v0, /device:TPU:3, one launch (start us, length us, event | category | flops | bytes accessed | tf_op | source)
XLA Modules:
  0.0 248.9 jit_solution(15624929625030205682)
XLA Ops:
  0.6 0.7 convert_element_type.3
  1.3 0.5 multiply_cosine_fusion
  1.9 0.8 pad_maximum_fusion.table_in
  2.6 243.9 %shard_map.68 = (bf16[256,3072]{1,0:T(8,128)(2,1)S(1)}, bf16[256,3584]{1,0:T(8,128)(2,1)S(1)}) custom-call(f32[256,128]{1,0:T(8,128)} %pad_maximum_fusion.table_in, bf16[256,2048]{1,0:T(8,128)(2,1)} %x_in.1, bf16[2048]{0:T(1024)(128)(2,1)} %gain_in.1, bf16[256,3072]{1,0:T(8,128)(2,1)} %wq_in.1, bf16[256,7168]{1,0:T(8,128)(2,1)} %wg_in.1), custom_call_target="tpu_custom_call" | custom-call | tf_op jit(solution)/shard_map/pallas_call | solution.py:359
  246.5 1.1 copy.9
  247.6 1.2 copy.10
  (1 shorter events, 0.0 us)
where the time goes:
time: 250 us; the launch traced here: 249 us
  Pallas kernels  244 us (98%)
    pallas_call x1, Pallas kernels, fused(): pl.pallas_call(functools.partial(kernel, plan), out_shape=(pltpu.VMEM((se...  244 us

commit v1 on v0

v1 whole, which is shorter than its diff:
```python
import functools

import jax
import jax.numpy as jnp
from jax import lax
from jax.experimental import pallas as pl
from jax.experimental.pallas import tpu as pltpu
from jax.sharding import PartitionSpec as P

QH = 32
KVH = 8
HD = 128
MESH = pl.DeviceIdType.MESH
CORES = 2
QUARTERS = 4
CHIPS = 8
WINDOW = 4
BACKLOG = 4
PIECES = 4
NEAR_FIRST = 0
WIDE = 2 * HD
OWN, ACROSS = (0, 1, 2, 3), (4, 5, 6, 7)

theta_base = 500000.0
norm_eps = 1e-05


def normalize(gathered, gain_row):
    values = gathered.astype(jnp.float32)
    mean_square = jnp.mean(values * values, axis=1, keepdims=True)
    return (values * lax.rsqrt(mean_square + norm_eps) * gain_row.astype(jnp.float32)).astype(
        jnp.bfloat16
    )


def frequencies():
    half_size = HD // 2
    return theta_base ** (-2.0 * jnp.arange(half_size, dtype=jnp.float32) / HD)


def rotary(joined_qkv, positions):
    row_count = joined_qkv.shape[0]
    per_group = QH // KVH + 2
    half_size = HD // 2
    head_view = joined_qkv.reshape(row_count, -1, per_group, HD)
    angles = positions.astype(jnp.float32)[:, None] * frequencies()[None, :]
    cosine = jnp.cos(angles)[:, None, None, :]
    sine_part = jnp.sin(angles)[:, None, None, :]
    leading = head_view[..., :half_size]
    trailing = head_view[..., half_size:]
    turned = jnp.concatenate(
        [leading * cosine - trailing * sine_part, trailing * cosine + leading * sine_part], axis=-1
    )
    rotated_mask = (jnp.arange(per_group) < per_group - 1)[None, None, :, None]
    return jnp.where(rotated_mask, turned, head_view).reshape(row_count, -1)


def contract_rows(chosen, piece):
    return jnp.dot(chosen, piece, preferred_element_type=jnp.float32)


def plain(positions, activations, norm_gain, qkv_weight, gate_up_weight):
    features, gains = (
        lax.all_gather(activations, "tp", axis=1, tiled=True),
        lax.all_gather(norm_gain, "tp", axis=0, tiled=True),
    )
    normed = normalize(features, gains)
    seq_count = normed.shape[0]
    qkv_partial = contract_rows(normed, lax.all_gather(qkv_weight, "rep", axis=0, tiled=True))
    gateup_partial = contract_rows(
        normed, lax.all_gather(gate_up_weight, "rep", axis=0, tiled=True)
    )
    qkv_out = rotary(qkv_partial, positions).astype(jnp.bfloat16)
    paired = gateup_partial.reshape(seq_count, 2, -1)
    hidden = (jax.nn.silu(paired[:, 0]) * paired[:, 1]).astype(jnp.bfloat16)
    return (qkv_out, hidden)


def kernel(plan, pos_in, freq_in, x_in, gain_in, wq_in, wg_in, q_out, h_out, *scratch):
    (seqs, feats, qcols, hcols) = plan
    n_q, n_h = qcols // WIDE, hcols // HD
    n = n_q + n_h
    (x_buf, t_buf, g_buf, f_buf, acc) = scratch[:5]
    p_buf = scratch[5:9]
    w_buf = scratch[9 : 9 + n]
    res = scratch[9 + n : 9 + 2 * n]
    (w_send, w_recv, f_send, f_recv, o_send, o_recv, a_send, a_recv, l_sem, ready) = scratch[9 + 2 * n :]
    last = n - 1

    rep, t = lax.axis_index("rep"), lax.axis_index("tp")
    core = rep % CORES
    chip = rep // CORES
    half = chip // QUARTERS
    quarter = chip % QUARTERS
    zl, y = quarter // 2, quarter % 2
    inner = (half + zl) % 2 == 1

    def flip_quarter(j):
        return (zl + j // 2 % 2) % 2 * 2 + (y + j % 2) % 2

    def flip(j):
        return (half + j // 4) % 2 * QUARTERS + flip_quarter(j)

    def dev(other_chip, other_core=None, other_t=None):
        return (
            other_chip * CORES + (core if other_core is None else other_core),
            t if other_t is None else other_t,
        )

    sibling = dev(chip, 1 - core)
    across = dev(chip, core, 1 - t)
    y_peer, z_peer, middle = dev(flip(1)), dev(flip(2)), dev(flip(6))

    def remote(src, dst, ssem, rsem, where):
        return pltpu.make_async_remote_copy(
            src_ref=src, dst_ref=dst, send_sem=ssem, recv_sem=rsem, device_id=where, device_id_type=MESH
        )

    def signal(sem, where):
        pl.semaphore_signal(sem, inc=1, device_id=where, device_id_type=MESH)

    def rows(index, count=1):
        return pl.ds(pl.multiple_of(index * seqs, seqs), count * seqs)

    def cols(base, width):
        return pl.ds(pl.multiple_of(base, HD), width)

    barrier = pltpu.get_barrier_semaphore()
    for where in (sibling, across, y_peer):
        signal(barrier, where)

    @pl.when(inner)
    def _():
        signal(barrier, middle)
        signal(barrier, z_peer)

    mine = cols(t * feats, feats)

    def mine_at(j):
        return x_buf.at[rows(flip_quarter(j)), mine]

    local = [
        pltpu.make_async_copy(x_in, mine_at(0), l_sem.at[0]),
        pltpu.make_async_copy(pos_in, p_buf[0], l_sem.at[1]),
        pltpu.make_async_copy(gain_in, g_buf.at[mine], l_sem.at[2]),
        pltpu.make_async_copy(freq_in, f_buf, l_sem.at[3]),
    ]
    for copy in local:
        copy.start()

    part_rows = seqs // PIECES

    def held(j, p):
        return x_buf.at[pl.ds(pl.multiple_of(flip_quarter(j) * seqs + p * part_rows, part_rows), part_rows), mine]

    def fresh(p):
        return x_in.at[p * part_rows : (p + 1) * part_rows, :]

    def act(n, src, j, where):
        return [
            remote(src(p), held(j, p), a_send.at[n, p], a_recv.at[n, p], where) for p in range(PIECES)
        ]

    z_x = act(0, fresh, 0, z_peer)
    y_x = act(1, fresh, 0, y_peer)
    y_two = act(2, functools.partial(held, 2), 2, y_peer)
    x_own = act(3, fresh, 0, across)
    x_two = act(4, functools.partial(held, 2), 2, across)
    x_three = act(5, functools.partial(held, 1), 1, across)
    x_four = act(6, functools.partial(held, 3), 3, across)
    x_gain = remote(gain_in, g_buf.at[mine], a_send.at[7, 0], a_recv.at[7, 0], across)
    p_far = [remote(pos_in, p_buf[j], a_send.at[7 + j, 0], a_recv.at[7 + j, 0], dev(flip(j))) for j in (1, 2, 3)]

    def sources(c, q):
        if c < n_q:
            return [wq_in.at[:, cols(q * qcols + c * WIDE, WIDE)]]
        at = q * hcols + (c - n_q) * HD
        return [wg_in.at[:, cols(part * hcols * QUARTERS + at, HD)] for part in range(2)]

    def slab(c, owner):
        return w_buf[c].at[rows(owner), :]

    def parts(c, owner):
        if c < n_q:
            return [slab(c, owner)]
        return [w_buf[c].at[rows(owner), part * HD : (part + 1) * HD] for part in range(2)]

    def weight_start(c, j):
        for src, dst in zip(sources(c, flip_quarter(j)), parts(c, rep)):
            remote(src, dst, w_send.at[c, j], w_recv.at[c, j], dev(flip(j))).start()

    def weight(c, j):
        place = slab(c, flip(j) * CORES + core)
        return remote(place, place, w_send.at[c, j], w_recv.at[c, j], dev(flip(j)))

    def start_own(c):
        for src, dst in zip(sources(c, quarter), parts(c, rep)):
            pltpu.make_async_copy(src, dst, l_sem.at[4 + c]).start()
            remote(src, dst, f_send.at[c, 0], f_recv.at[c, 0], sibling).start()

    def own_wait(c):
        place = slab(c, rep)
        pltpu.make_async_copy(place, place, l_sem.at[4 + c]).wait()

    def passed(c, j):
        place = slab(c, flip(j) * CORES + core)
        return remote(place, place, f_send.at[c, j], f_recv.at[c, j], sibling)

    def passed_in(c, j):
        place = slab(c, flip(j) * CORES + 1 - core)
        return remote(place, place, f_send.at[c, j], f_recv.at[c, j], sibling)

    def start_near(c):
        for j in OWN[1:]:
            weight_start(c, j)
        start_own(c)

    def start_far(c):
        for j in ACROSS:
            weight_start(c, j)

    def take(c, js):
        for j in js:
            if j:
                weight(c, j).wait_recv()
                passed(c, j).start()

    def settle(c, js):
        for j in js:
            if j == 0:
                own_wait(c)
            passed_in(c, j).wait_recv()

    def advance(c):
        if c + WINDOW < n:
            for j in ACROSS:
                weight(c, j).wait_send()
                weight_start(c + WINDOW, j)

    pl.semaphore_wait(barrier, 4)

    @pl.when(inner)
    def _():
        weight_start(0, 6)

    for copy in (*x_own, *y_x, x_gain):
        copy.start()

    @pl.when(inner)
    def _():
        pl.semaphore_wait(ready.at[0], 1)
        signal(ready.at[1], middle)
        for copy in z_x:
            copy.start()
        pl.semaphore_wait(ready.at[1], 1)
        signal(ready.at[2], z_peer)

    @pl.when(jnp.logical_not(inner))
    def _():
        signal(ready.at[0], z_peer)
        for copy in z_x:
            copy.start()
        pl.semaphore_wait(ready.at[2], 1)
        weight_start(0, 6)

    for copy in p_far:
        copy.start()
    for j in (4, 5, 7):
        weight_start(0, j)
    for c in range(1, WINDOW):
        start_far(c)
    for c in range(NEAR_FIRST):
        start_near(c)
    for p in range(PIECES):
        z_x[p].wait_recv()
        x_two[p].start()
        y_two[p].start()
    for p in range(PIECES):
        y_x[p].wait_recv()
        x_three[p].start()
    for c in range(NEAR_FIRST, n):
        start_near(c)
    for p in range(PIECES):
        y_two[p].wait_recv()
        x_four[p].start()
    for c in range(BACKLOG):
        take(c, OWN + ACROSS)
        advance(c)

    for copy in local:
        copy.wait()
    for copy in p_far:
        copy.wait_recv()

    freq = f_buf[...]
    for j in range(QUARTERS):
        for s in range(seqs // HD):
            line = p_buf[j][s * HD : (s + 1) * HD].astype(jnp.float32)[None, :]
            angles = jnp.transpose(jnp.broadcast_to(line, (HD, HD))) * freq
            at_rows = pl.ds(pl.multiple_of(flip_quarter(j) * seqs + s * HD, HD), HD)
            t_buf[at_rows, :HD] = jnp.cos(angles)
            lane = lax.broadcasted_iota(jnp.int32, angles.shape, 1)
            sines = jnp.sin(angles)
            t_buf[at_rows, HD:] = jnp.where(lane < HD // 2, -sines, sines)

    tall = 32
    x_gain.wait_recv()
    gain_row = g_buf[...].astype(jnp.float32)[None, :]

    for j, copies in ((0, x_own), (2, x_two), (1, x_three), (3, x_four)):
        for copy in copies:
            copy.wait_recv()
        for copy in {0: (*z_x, *y_x, *x_own, x_gain, *p_far), 2: (*y_two, *x_two), 1: x_three, 3: x_four}[j]:
            copy.wait_send()

        @pl.loop(0, seqs // tall)
        def _(i):
            at_rows = pl.ds(pl.multiple_of(flip_quarter(j) * seqs + i * tall, tall), tall)
            values = x_buf[at_rows, :].astype(jnp.float32)
            mean_square = jnp.mean(values * values, axis=1, keepdims=True)
            x_buf[at_rows, :] = (values * lax.rsqrt(mean_square + norm_eps) * gain_row).astype(jnp.bfloat16)

    total = QUARTERS * seqs
    per_group = QH // KVH + 2
    deep = 2 * seqs

    def turn(c, at_rows, wide):
        for s in range(WIDE // HD):
            head = wide[:, s * HD : (s + 1) * HD]
            if (c * (WIDE // HD) + s) % per_group < per_group - 1:
                head = head * t_buf[at_rows, :HD] + pltpu.roll(head, HD // 2, 1) * t_buf[at_rows, HD:]
            res[c][at_rows, s * HD : (s + 1) * HD] = head.astype(jnp.bfloat16)

    def gated(c, at_rows, wide):
        gate, up = wide[:, :HD], wide[:, HD:]
        res[c][at_rows, :] = (gate / (1.0 + jnp.exp(-gate)) * up).astype(jnp.bfloat16)

    def compute(c):
        @pl.loop(0, total // deep)
        def _(i):
            at_rows = pl.ds(pl.multiple_of(i * deep, deep), deep)
            wide = jnp.dot(x_buf[at_rows, :], w_buf[c][...], preferred_element_type=jnp.float32)
            (turn if c < n_q else gated)(c, at_rows, wide)

    def back(c, j):
        src = res[c].at[rows(flip_quarter(j)), :]
        if c < n_q:
            dst = q_out.at[:, cols(quarter * qcols + c * WIDE, WIDE)]
        else:
            dst = h_out.at[:, cols(quarter * hcols + (c - n_q) * HD, HD)]
        return src, dst

    def back_send(c, j):
        src, dst = back(c, j)
        return remote(src, dst, o_send.at[c, j], o_recv.at[c, j], dev(flip(j)))

    def back_from(c, j):
        mover = flip_quarter(j)
        if c < n_q:
            dst = q_out.at[:, cols(mover * qcols + c * WIDE, WIDE)]
        else:
            dst = h_out.at[:, cols(mover * hcols + (c - n_q) * HD, HD)]
        return remote(dst, dst, o_send.at[c, j], o_recv.at[c, j], dev(flip(j)))

    def back_own(c):
        return pltpu.make_async_copy(*back(c, 0), o_send.at[c, 0])

    def ship(c, js=(3, 1, 2, 0)):
        for j in js:
            (back_send(c, j) if j else back_own(c)).start()

    for c in range(n - 1):
        if c >= BACKLOG:
            take(c, OWN + ACROSS)
            advance(c)
        settle(c, OWN + ACROSS)
        compute(c)
        ship(c)

    deep_half = QUARTERS * CORES * seqs
    near = pl.ds(pl.multiple_of(half * deep_half, deep_half), deep_half)
    far = pl.ds(pl.multiple_of((1 - half) * deep_half, deep_half), deep_half)
    take(last, OWN)
    settle(last, OWN)

    @pl.loop(0, total // deep)
    def _(i):
        at_rows = pl.ds(pl.multiple_of(i * deep, deep), deep)
        acc[at_rows, :] = jnp.dot(x_buf[at_rows, near], w_buf[last][near, :], preferred_element_type=jnp.float32)
    take(last, ACROSS)
    settle(last, ACROSS)
    for j in (3, 1, 2, 0):
        at_rows = rows(flip_quarter(j))
        gated(
            last,
            at_rows,
            acc[at_rows, :]
            + jnp.dot(x_buf[at_rows, far], w_buf[last][far, :], preferred_element_type=jnp.float32),
        )
        ship(last, (j,))
    for c in range(n):
        for j in OWN + ACROSS:
            if j and (c + WINDOW >= n or j < QUARTERS):
                weight(c, j).wait_send()
            if j:
                passed(c, j).wait_send()
        own_slab = slab(c, rep)
        remote(own_slab, own_slab, f_send.at[c, 0], f_recv.at[c, 0], sibling).wait_send()
        for j in OWN[1:]:
            back_send(c, j).wait_send()
            back_from(c, j).wait_recv()
        back_own(c).wait()


def fused(positions, activations, norm_gain, qkv_weight, gate_up_weight):
    seqs, feats = activations.shape
    depth, qkv_cols = qkv_weight.shape
    qcols = qkv_cols // QUARTERS
    hcols = gate_up_weight.shape[1] // 2 // QUARTERS
    n_q, n_h = qcols // WIDE, hcols // HD
    n = n_q + n_h
    rank = CHIPS * CORES
    freq = frequencies()
    freq = jnp.concatenate([freq, freq])[None, :]
    bf16, f32 = jnp.bfloat16, jnp.float32
    dma = pltpu.SemaphoreType.DMA
    total = QUARTERS * seqs
    scratch = [
        pltpu.VMEM((total, 2 * feats), bf16),
        pltpu.VMEM((total, 2 * HD), f32),
        pltpu.VMEM((2 * feats,), bf16),
        pltpu.VMEM((1, HD), f32),
        pltpu.VMEM((total, WIDE), f32),
        *[pltpu.VMEM((seqs,), jnp.int32) for _ in range(QUARTERS)],
        *[pltpu.VMEM((rank * depth, WIDE), bf16) for _ in range(n)],
        *[pltpu.VMEM((total, WIDE), bf16) for _ in range(n_q)],
        *[pltpu.VMEM((total, HD), bf16) for _ in range(n_h)],
        dma((n, CHIPS)),
        dma((n, CHIPS)),
        dma((n, CHIPS)),
        dma((n, CHIPS)),
        dma((n, QUARTERS)),
        dma((n, QUARTERS)),
        dma((11, PIECES)),
        dma((11, PIECES)),
        dma((4 + n,)),
        pltpu.SemaphoreType.REGULAR((3,)),
    ]
    plan = (seqs, feats, qcols, hcols)
    anywhere = pl.BlockSpec(memory_space=pl.ANY)
    return pl.pallas_call(
        functools.partial(kernel, plan),
        out_shape=(
            pltpu.VMEM((seqs, qkv_cols), bf16),
            pltpu.VMEM((seqs, hcols * QUARTERS), bf16),
        ),
        in_specs=[anywhere] * 6,
        out_specs=(pl.BlockSpec(memory_space=pltpu.VMEM), pl.BlockSpec(memory_space=pltpu.VMEM)),
        scratch_shapes=scratch,
        compiler_params=pltpu.CompilerParams(
            collective_id=0, has_side_effects=True, vmem_limit_bytes=60 * 1024 * 1024
        ),
    )(positions, freq, activations, norm_gain, qkv_weight, gate_up_weight)


def per_device(reps, tps, positions, activations, norm_gain, qkv_weight, gate_up_weight):
    seqs, depth = activations.shape[0], qkv_weight.shape[0]
    fits = (
        reps == CHIPS * CORES
        and tps == 2
        and seqs == depth
        and seqs % HD == 0
        and qkv_weight.shape[1] % (QUARTERS * (QH // KVH + 2) * HD) == 0
        and gate_up_weight.shape[1] % (2 * QUARTERS * HD) == 0
    )
    step = fused if fits else plain
    return step(positions, activations, norm_gain, qkv_weight, gate_up_weight)


def solution(mesh):
    placed = (P("rep"), P("rep", "tp"), P("tp"), P("rep", "tp"), P("rep", "tp"))
    return jax.shard_map(
        functools.partial(per_device, mesh.shape["rep"], mesh.shape["tp"]),
        mesh=mesh,
        in_specs=placed,
        out_specs=(P("rep", "tp"), P("rep", "tp")),
        check_vma=False,
    )
```

time: 250 us -> 248 us (level)
  no operation moved by 1% of the time
where the time goes in v1:
time: 248 us
  Pallas kernels  244 us (98%)
    pallas_call x1, Pallas kernels, fused(): pl.pallas_call(functools.partial(kernel, plan), out_shape=(pltpu.VMEM((se...  244 us

profile of v1, /device:TPU:3, one launch (start us, length us, event | category | flops | bytes accessed | tf_op | source)
XLA Modules:
  0.0 247.6 jit_solution(16196966933765341645)
XLA Ops:
  0.6 0.6 maximum_bitcast_fusion.freq_in
  1.2 244.0 %shard_map.68 = (bf16[256,3072]{1,0:T(8,128)(2,1)S(1)}, bf16[256,3584]{1,0:T(8,128)(2,1)S(1)}) custom-call(s32[256]{0:T(256)} %pos_in.1, f32[1,128]{1,0:T(1,128)} %maximum_bitcast_fusion.freq_in, bf16[256,2048]{1,0:T(8,128)(2,1)} %x_in.1, bf16[2048]{0:T(1024)(128)(2,1)} %gain_in.1, bf16[256,3072]{1,0:T(8,128)(2,1)} %wq_in.1, bf16[256,7168]{1,0:T(8,128)(2,1)} %wg_in.1), custom_call_target="tpu_custom_call" | custom-call | tf_op jit(solution)/shard_map/pallas_call | solution.py:451
  245.3 1.1 copy.9
  246.4 1.2 copy.10
  (1 shorter events, 0.0 us)

commit v2 on v1

--- a/solution.py
+++ b/solution.py
@@ -1,4 +1,5 @@
 import functools
+import math
 
 import jax
 import jax.numpy as jnp
@@ -19,7 +20,10 @@
 PIECES = 4
 NEAR_FIRST = 0
 WIDE = 2 * HD
-OWN, ACROSS = (0, 1, 2, 3), (4, 5, 6, 7)
+ACROSS = (4, 5, 6, 7)
+NEAR_LEAD = 0
+EARLY = 2
+OWN = (0, 1, 2, 3)
 
 theta_base = 500000.0
 norm_eps = 1e-05
@@ -76,15 +80,15 @@
     return (qkv_out, hidden)
 
 
-def kernel(plan, pos_in, freq_in, x_in, gain_in, wq_in, wg_in, q_out, h_out, *scratch):
+def kernel(plan, pos_in, x_in, gain_in, wq_in, wg_in, q_out, h_out, *scratch):
     (seqs, feats, qcols, hcols) = plan
     n_q, n_h = qcols // WIDE, hcols // HD
     n = n_q + n_h
-    (x_buf, t_buf, g_buf, f_buf, acc) = scratch[:5]
-    p_buf = scratch[5:9]
-    w_buf = scratch[9 : 9 + n]
-    res = scratch[9 + n : 9 + 2 * n]
-    (w_send, w_recv, f_send, f_recv, o_send, o_recv, a_send, a_recv, l_sem, ready) = scratch[9 + 2 * n :]
+    (x_buf, t_buf, g_buf, acc) = scratch[:4]
+    p_buf = scratch[4:8]
+    w_buf = scratch[8 : 8 + n]
+    res = scratch[8 + n : 8 + 2 * n]
+    (w_send, w_recv, f_send, f_recv, o_send, o_recv, a_send, a_recv, l_sem, ready) = scratch[8 + 2 * n :]
     last = n - 1
 
     rep, t = lax.axis_index("rep"), lax.axis_index("tp")
@@ -143,7 +147,6 @@
         pltpu.make_async_copy(x_in, mine_at(0), l_sem.at[0]),
         pltpu.make_async_copy(pos_in, p_buf[0], l_sem.at[1]),
         pltpu.make_async_copy(gain_in, g_buf.at[mine], l_sem.at[2]),
-        pltpu.make_async_copy(freq_in, f_buf, l_sem.at[3]),
     ]
     for copy in local:
         copy.start()
@@ -236,12 +239,18 @@
             for j in ACROSS:
                 weight(c, j).wait_send()
                 weight_start(c + WINDOW, j)
+                near = j - 4
+                if near and c + WINDOW + NEAR_LEAD < n:
+                    weight_start(c + WINDOW + NEAR_LEAD, near)
+            if c + WINDOW + NEAR_LEAD < n:
+                start_own(c + WINDOW + NEAR_LEAD)
 
     pl.semaphore_wait(barrier, 4)
 
     @pl.when(inner)
     def _():
-        weight_start(0, 6)
+        for c in range(EARLY):
+            weight_start(c, 6)
 
     for copy in (*x_own, *y_x, x_gain):
         copy.start()
@@ -261,16 +270,18 @@
         for copy in z_x:
             copy.start()
         pl.semaphore_wait(ready.at[2], 1)
-        weight_start(0, 6)
+        for c in range(EARLY):
+            weight_start(c, 6)
 
     for copy in p_far:
         copy.start()
-    for j in (4, 5, 7):
-        weight_start(0, j)
-    for c in range(1, WINDOW):
-        start_far(c)
+    for c in range(WINDOW):
+        for j in ACROSS:
+            if j != 6 or c >= EARLY:
+                weight_start(c, j)
     for c in range(NEAR_FIRST):
         start_near(c)
+
     for p in range(PIECES):
         z_x[p].wait_recv()
         x_two[p].start()
@@ -279,7 +290,8 @@
         y_x[p].wait_recv()
         x_three[p].start()
     for c in range(NEAR_FIRST, n):
-        start_near(c)
+        if c < WINDOW + NEAR_LEAD:
+            start_near(c)
     for p in range(PIECES):
         y_two[p].wait_recv()
         x_four[p].start()
@@ -292,7 +304,8 @@
     for copy in p_far:
         copy.wait_recv()
 
-    freq = f_buf[...]
+    entry = lax.broadcasted_iota(jnp.int32, (1, HD), 1) % (HD // 2)
+    freq = jnp.exp(entry.astype(jnp.float32) * (-2.0 / HD * math.log(theta_base)))
     for j in range(QUARTERS):
         for s in range(seqs // HD):
             line = p_buf[j][s * HD : (s + 1) * HD].astype(jnp.float32)[None, :]
@@ -387,6 +400,7 @@
     def _(i):
         at_rows = pl.ds(pl.multiple_of(i * deep, deep), deep)
         acc[at_rows, :] = jnp.dot(x_buf[at_rows, near], w_buf[last][near, :], preferred_element_type=jnp.float32)
+
     take(last, ACROSS)
     settle(last, ACROSS)
     for j in (3, 1, 2, 0):
@@ -398,6 +412,7 @@
             + jnp.dot(x_buf[at_rows, far], w_buf[last][far, :], preferred_element_type=jnp.float32),
         )
         ship(last, (j,))
+
     for c in range(n):
         for j in OWN + ACROSS:
             if j and (c + WINDOW >= n or j < QUARTERS):
@@ -420,8 +435,6 @@
     n_q, n_h = qcols // WIDE, hcols // HD
     n = n_q + n_h
     rank = CHIPS * CORES
-    freq = frequencies()
-    freq = jnp.concatenate([freq, freq])[None, :]
     bf16, f32 = jnp.bfloat16, jnp.float32
     dma = pltpu.SemaphoreType.DMA
     total = QUARTERS * seqs
@@ -429,7 +442,6 @@
         pltpu.VMEM((total, 2 * feats), bf16),
         pltpu.VMEM((total, 2 * HD), f32),
         pltpu.VMEM((2 * feats,), bf16),
-        pltpu.VMEM((1, HD), f32),
         pltpu.VMEM((total, WIDE), f32),
         *[pltpu.VMEM((seqs,), jnp.int32) for _ in range(QUARTERS)],
         *[pltpu.VMEM((rank * depth, WIDE), bf16) for _ in range(n)],
@@ -454,13 +466,13 @@
             pltpu.VMEM((seqs, qkv_cols), bf16),
             pltpu.VMEM((seqs, hcols * QUARTERS), bf16),
         ),
-        in_specs=[anywhere] * 6,
+        in_specs=[anywhere] * 5,
         out_specs=(pl.BlockSpec(memory_space=pltpu.VMEM), pl.BlockSpec(memory_space=pltpu.VMEM)),
         scratch_shapes=scratch,
         compiler_params=pltpu.CompilerParams(
             collective_id=0, has_side_effects=True, vmem_limit_bytes=60 * 1024 * 1024
         ),
-    )(positions, freq, activations, norm_gain, qkv_weight, gate_up_weight)
+    )(positions, activations, norm_gain, qkv_weight, gate_up_weight)
 
 
 def per_device(reps, tps, positions, activations, norm_gain, qkv_weight, gate_up_weight):

time: 248 us -> 246 us (level)
  no operation moved by 1% of the time
where the time goes in v2:
time: 246 us
  Pallas kernels  243 us (99%)
    pallas_call x1, Pallas kernels, fused(): pl.pallas_call(functools.partial(kernel, plan), out_shape=(pltpu.VMEM((se...  243 us

profile of v2, /device:TPU:3, one launch (start us, length us, event | category | flops | bytes accessed | tf_op | source)
XLA Modules:
  0.0 246.1 jit_solution(14894984708416434017)
XLA Ops:
  0.6 243.1 %shard_map.68 = (bf16[256,3072]{1,0:T(8,128)(2,1)S(1)}, bf16[256,3584]{1,0:T(8,128)(2,1)S(1)}) custom-call(s32[256]{0:T(256)} %pos_in.1, bf16[256,2048]{1,0:T(8,128)(2,1)} %x_in.1, bf16[2048]{0:T(1024)(128)(2,1)} %gain_in.1, bf16[256,3072]{1,0:T(8,128)(2,1)} %wq_in.1, bf16[256,7168]{1,0:T(8,128)(2,1)} %wg_in.1), custom_call_target="tpu_custom_call" | custom-call | tf_op jit(solution)/shard_map/pallas_call | solution.py:463
  243.7 1.1 copy.9
  244.8 1.2 copy.10
